TPU v7x, 32 devices: a whole 2x2x4 slice. The times are simulated.
32 devices in a mesh: groups: 2 (over y), pair: 4 (over z), tp: 4 (over x, core).
Axes of the slice: x: 2, y: 2, z: 4, core: 2. Of those that a mesh axis runs over, the one named last changes fastest.
Arguments:
- prompt_keys: bfloat16 [8, 1536, 8, 128], P(('groups', 'pair'), None, 'tp'), parts along dimension 0, may hold values from -6 to 6
- prompt_values: bfloat16 [8, 1536, 8, 128], P(('groups', 'pair'), None, 'tp'), parts along dimension 0, may hold values from -6 to 6
- span_queries: bfloat16 [8, 512, 64, 128], P(('groups', 'pair'), None, 'tp'), parts along dimension 0, may hold values from -1024 to 1024
- span_keys: bfloat16 [8, 512, 8, 128], P(('groups', 'pair'), None, 'tp'), parts along dimension 0, may hold values from -6 to 6
- span_values: bfloat16 [8, 512, 8, 128], P(('groups', 'pair'), None, 'tp'), parts along dimension 0, may hold values from -6 to 6
- prefill_residual: bfloat16 [8, 512, 8192], P(('groups', 'pair'), None, 'tp'), parts along dimension 0, may hold values from -8 to 8
- decode_queries: bfloat16 [8, 2, 32, 64, 128], P(('groups', 'pair'), None, None, 'tp'), parts along dimension 0, may hold values from -1024 to 1024
- decode_keys: bfloat16 [8, 2, 32, 8, 128], P(('groups', 'pair'), None, None, 'tp'), parts along dimension 0, may hold values from -16 to 16
- decode_values: bfloat16 [8, 2, 32, 8, 128], P(('groups', 'pair'), None, None, 'tp'), parts along dimension 0, may hold values from -6 to 6
- decode_residual: bfloat16 [8, 2, 32, 8192], P(('groups', 'pair'), None, None, 'tp'), parts along dimension 0, may hold values from -8 to 8
- cursor: int32 [8, 32], P(('groups', 'pair')), parts along dimension 0, may hold values from 1024 to 2048
- norm_gain: bfloat16 [8192], P('tp'), may hold values from 0.25 to 1.75
Outputs:
- prefill_normed: bfloat16 [8, 512, 8192], P(('groups', 'pair'), None, 'tp'), parts along dimension 0
- handed_keys: bfloat16 [8, 2048, 8, 128], P(('groups', 'pair'), None, 'tp'), parts along dimension 0
- handed_values: bfloat16 [8, 2048, 8, 128], P(('groups', 'pair'), None, 'tp'), parts along dimension 0
- decode_normed: bfloat16 [8, 2, 32, 8192], P(('groups', 'pair'), None, None, 'tp'), parts along dimension 0
There are 2 independent parts, one for each index of `groups`. A program takes and returns all parts, laid end to end along the dimension named above; an argument that names none is the same for every part. Nothing has to cross between parts.
All inputs are finite; a program needn't handle non-finite values.
Results may differ from a plain program's by a relative error of at most 0.0034.
Values may be sent and summed in bfloat16 or wider, within the bound.
A program may use at most 128 MiB of HBM per device.

v0:
```python
import functools

import jax
import jax.numpy as jnp
from jax import lax
from jax.experimental import pallas as pl
from jax.experimental.pallas import tpu as pltpu
from jax.sharding import PartitionSpec as P


epsilon = 1e-05
FIRST = ("half_pk", "half_sk", "half_pv", "half_sv")
SECOND = ("full_pk", "full_sk", "full_pv", "full_sv", "full_tv")
CROSS = FIRST[2:] + SECOND[2:]
NT = (((1,), (1,)), ((), ()))
MESH = pl.DeviceIdType.MESH


def routes(count):
    half, quarter = count // 2, count // 4
    if count % 4:
        first = [(place, (place + half) % count) for place in range(count)]
        return first, [(place, place) for place in range(count)]
    first, second = [], []
    for place in range(count):
        outer = place < quarter or place >= count - quarter
        step = quarter if outer else half
        first.append((place, place + step if place < half else place - step))
        second.append((place, place if outer else place + quarter if place < half else place - quarter))
    return first, second


def crossed(value, pairs):
    wide = lax.axis_size("tp")
    other = [t if wide % 2 else t + 1 - 2 * (t % 2) for t in range(wide)]
    both = [(a * wide + t, b * wide + other[t]) for a, b in pairs for t in range(wide)]
    return lax.ppermute(value, ("pair", "tp"), both)


def prefill_kernel(block, past, scale, q_ref, k_ref, v_ref, res_ref, hid_ref, sq_ref):
    span, _ = q_ref.shape[1:]

    @pl.when(pl.program_id(0) == 0)
    def _():
        sq_ref[...] = jnp.zeros_like(sq_ref)

    for start in range(0, span, block):
        rows = slice(start, start + block)
        reach = past + start + block
        scores = lax.dot_general(
            q_ref[0, rows, :], k_ref[0, :reach, :], NT, preferred_element_type=jnp.float32
        )
        row = lax.broadcasted_iota(jnp.int32, (block, block), 0)
        col = lax.broadcasted_iota(jnp.int32, (block, block), 1)
        last = jnp.where(col <= row, scores[:, reach - block :], -jnp.inf)
        scores = jnp.concatenate([scores[:, : reach - block], last], axis=1)
        peak = jnp.max(scores, axis=1, keepdims=True)
        weights = jnp.exp((scores - peak) * scale)
        total = jnp.sum(weights, axis=1, keepdims=True)
        mixed = jnp.dot(
            weights.astype(jnp.bfloat16), v_ref[0, :reach, :], preferred_element_type=jnp.float32
        )
        hidden = mixed / total + res_ref[rows, :].astype(jnp.float32)
        hid_ref[rows, :] = hidden
        sq_ref[rows, :] += hidden * hidden


def prefill(queries, keys, values, residual, first, last):
    heads, span, head = queries.shape
    key_heads, positions, _ = keys.shape
    group = heads // key_heads
    block = min(256, span)
    return pl.pallas_call(
        functools.partial(prefill_kernel, block, positions - span, head ** (-0.5)),
        grid=(last - first,),
        in_specs=[
            pl.BlockSpec((1, span, head), lambda h: (first + h, 0, 0)),
            pl.BlockSpec((1, positions, head), lambda h: ((first + h) // group, 0, 0)),
            pl.BlockSpec((1, positions, head), lambda h: ((first + h) // group, 0, 0)),
            pl.BlockSpec((span, head), lambda h: (0, first + h)),
        ],
        out_specs=[
            pl.BlockSpec((span, head), lambda h: (0, h)),
            pl.BlockSpec((span, head), lambda h: (0, 0)),
        ],
        out_shape=[
            jax.ShapeDtypeStruct((span, (last - first) * head), jnp.float32),
            jax.ShapeDtypeStruct((span, head), jnp.float32),
        ],
        compiler_params=pltpu.CompilerParams(vmem_limit_bytes=40 * 2**20),
        cost_estimate=pl.CostEstimate(
            flops=8 * (last - first) * span * positions * head,
            bytes_accessed=8 * 2**20,
            transcendentals=(last - first) * span * positions,
        ),
        name="prefill",
    )(queries, keys, values, residual)


def weigh_kernel(
    scale, key_heads, steps, q_ref, pk_ref, sk_ref, dk_ref, dv_ref, cur_ref,
    w_ref, last_ref, inv_ref, own_ref, hk_ref,
):
    g = pl.program_id(0)
    first = jnp.logical_and(g == 0, pl.program_id(1) == 0)
    past = pk_ref.shape[0]

    @pl.when(first)
    def _():
        hk_ref[:past, :] = pk_ref[...]
        hk_ref[past:, :] = sk_ref[...]

    q = q_ref[0]
    rows = q.shape[0]
    scores = jnp.concatenate(
        [
            lax.dot_general(q, pk_ref[...], NT, preferred_element_type=jnp.float32),
            lax.dot_general(q, sk_ref[...], NT, preferred_element_type=jnp.float32),
        ],
        axis=1,
    )
    col = lax.broadcasted_iota(jnp.int32, scores.shape, 1)
    seen = jnp.logical_and(col % key_heads == g, col < cur_ref[...] * key_heads)
    scores = jnp.where(seen, scores, -jnp.inf)
    peak = jnp.max(scores, axis=1, keepdims=True)
    count = dk_ref.shape[2]
    copies = rows // count
    step = lax.broadcasted_iota(jnp.int32, (rows, 1), 0) // count % steps
    wide = q.astype(jnp.float32)
    own_scores = []
    for u in range(steps):
        key = jnp.concatenate([dk_ref[0, u].astype(jnp.float32)] * copies, axis=0)
        own = jnp.sum(wide * key, axis=1, keepdims=True)
        own = jnp.where(step >= u, own, -jnp.inf)
        own_scores.append(own)
        peak = jnp.maximum(peak, own)
    weights = jnp.exp((scores - peak) * scale)
    total = jnp.sum(weights, axis=1, keepdims=True)
    rounded = weights.astype(jnp.bfloat16)
    w_ref[0] = rounded[:, : w_ref.shape[2]]
    last_ref[0] = rounded[:, w_ref.shape[2] :]
    mixed = jnp.zeros(wide.shape, jnp.float32)
    for u in range(steps):
        value = jnp.concatenate([dv_ref[0, u].astype(jnp.float32)] * copies, axis=0)
        weight = jnp.exp((own_scores[u] - peak) * scale)
        total = total + weight
        mixed = mixed + weight.astype(jnp.bfloat16).astype(jnp.float32) * value
    inv_ref[0] = jnp.broadcast_to(1.0 / total, wide.shape)
    own_ref[0] = mixed


def weigh(queries, prompt_keys, span_keys, own_keys, own_values, reach, ending):
    key_heads, rows, head = queries.shape
    _, steps, count, _ = own_keys.shape
    past, span = prompt_keys.shape[0], span_keys.shape[0]
    block = reach.shape[0]
    return pl.pallas_call(
        functools.partial(weigh_kernel, head ** (-0.5), key_heads, steps),
        grid=(key_heads, rows // block),
        in_specs=[
            pl.BlockSpec((1, block, head), lambda g, i: (g, i, 0)),
            pl.BlockSpec((past, head), lambda g, i: (0, 0)),
            pl.BlockSpec((span, head), lambda g, i: (0, 0)),
            pl.BlockSpec((1, steps, count, head), lambda g, i: (g, 0, 0, 0)),
            pl.BlockSpec((1, steps, count, head), lambda g, i: (g, 0, 0, 0)),
            pl.BlockSpec((block, 1), lambda g, i: (0, 0)),
        ],
        out_specs=[
            pl.BlockSpec((1, block, past + span - ending), lambda g, i: (g, i, 0)),
            pl.BlockSpec((1, block, ending), lambda g, i: (g, i, 0)),
            pl.BlockSpec((1, block, head), lambda g, i: (g, i, 0)),
            pl.BlockSpec((1, block, head), lambda g, i: (g, i, 0)),
            pl.BlockSpec((past + span, head), lambda g, i: (0, 0)),
        ],
        out_shape=[
            jax.ShapeDtypeStruct((key_heads, rows, past + span - ending), jnp.bfloat16),
            jax.ShapeDtypeStruct((key_heads, rows, ending), jnp.bfloat16),
            jax.ShapeDtypeStruct((key_heads, rows, head), jnp.float32),
            jax.ShapeDtypeStruct((key_heads, rows, head), jnp.float32),
            jax.ShapeDtypeStruct((past + span, head), jnp.bfloat16),
        ],
        compiler_params=pltpu.CompilerParams(vmem_limit_bytes=40 * 2**20),
        cost_estimate=pl.CostEstimate(
            flops=4 * key_heads * rows * (past + span) * head,
            bytes_accessed=16 * 2**20,
            transcendentals=key_heads * rows * (past + span),
        ),
        name="weigh",
    )(queries, prompt_keys, span_keys, own_keys, own_values, reach)


def mix_kernel(w_ref, v_ref, own_ref, acc_ref, hv_ref):
    @pl.when(pl.program_id(0) == 0)
    def _():
        hv_ref[...] = v_ref[...]

    acc_ref[0] = own_ref[0] + jnp.dot(w_ref[0], v_ref[...], preferred_element_type=jnp.float32)


def mix(weights, prompt_values, own, both):
    key_heads, rows, _ = weights.shape
    past, head = prompt_values.shape
    return pl.pallas_call(
        mix_kernel,
        grid=(key_heads,),
        in_specs=[
            pl.BlockSpec((1, rows, past), lambda g: (g, 0, 0)),
            pl.BlockSpec((past, head), lambda g: (0, 0)),
            pl.BlockSpec((1, rows, head), lambda g: (g, 0, 0)),
        ],
        out_specs=[
            pl.BlockSpec((1, rows, head), lambda g: (g, 0, 0)),
            pl.BlockSpec((past, head), lambda g: (0, 0)),
        ],
        out_shape=[
            jax.ShapeDtypeStruct((key_heads, rows, head), jnp.float32),
            jax.ShapeDtypeStruct((both, head), jnp.bfloat16),
        ],
        compiler_params=pltpu.CompilerParams(vmem_limit_bytes=40 * 2**20),
        cost_estimate=pl.CostEstimate(
            flops=4 * key_heads * rows * past * head, bytes_accessed=8 * 2**20, transcendentals=0
        ),
        name="mix",
    )(weights, prompt_values, own)


def gather_kernel(w_ref, v_ref, acc_ref, inv_ref, res_ref, part_ref):
    mixed = acc_ref[0] + jnp.dot(w_ref[0], v_ref[...], preferred_element_type=jnp.float32)
    mixed = mixed * inv_ref[0]
    count = res_ref.shape[0]
    head = mixed.shape[1]
    for h in range(mixed.shape[0] // count):
        columns = slice(h * head, (h + 1) * head)
        part_ref[:, columns] = mixed[h * count : (h + 1) * count] + res_ref[:, columns].astype(jnp.float32)


def gather(weights, span_values, acc, inverse, residual):
    key_heads, rows, columns = weights.shape
    span, head = span_values.shape
    count, width = residual.shape
    at = columns // span - 1
    return pl.pallas_call(
        gather_kernel,
        grid=(key_heads,),
        in_specs=[
            pl.BlockSpec((1, rows, span), lambda g: (g, 0, at)),
            pl.BlockSpec((span, head), lambda g: (0, 0)),
            pl.BlockSpec((1, rows, head), lambda g: (g, 0, 0)),
            pl.BlockSpec((1, rows, head), lambda g: (g, 0, 0)),
            pl.BlockSpec((count, width // key_heads), lambda g: (0, g)),
        ],
        out_specs=pl.BlockSpec((count, width // key_heads), lambda g: (0, g)),
        out_shape=jax.ShapeDtypeStruct((count, width), jnp.float32),
        compiler_params=pltpu.CompilerParams(vmem_limit_bytes=40 * 2**20),
        cost_estimate=pl.CostEstimate(
            flops=4 * key_heads * rows * span * head, bytes_accessed=6 * 2**20, transcendentals=0
        ),
        name="gather",
    )(weights, span_values, acc, inverse, residual)


def close_kernel(
    w_ref, v_ref, part_ref, inv_ref, hid_ref, sum_ref, mine, others, send_sem, recv_sem
):
    devices, me = lax.axis_size("tp"), lax.axis_index("tp")
    ahead = [{"tp": lax.rem(me + k, devices)} for k in range(1, devices)]
    barrier = pltpu.get_barrier_semaphore()
    for peer in ahead:
        pl.semaphore_signal(barrier, inc=1, device_id=peer, device_id_type=MESH)

    key_heads, rows, _ = w_ref.shape
    count = part_ref.shape[0]
    head = v_ref.shape[1]
    squares = jnp.zeros((count, head), jnp.float32)
    for g in range(key_heads):
        mixed = jnp.dot(w_ref[g], v_ref[...], preferred_element_type=jnp.float32) * inv_ref[g]
        for h in range(rows // count):
            at = (g * (rows // count) + h) * head
            hidden = part_ref[:, at : at + head] + mixed[h * count : (h + 1) * count]
            hid_ref[:, at : at + head] = hidden
            squares = squares + hidden * hidden
    sums = jnp.sum(squares, axis=1, keepdims=True)
    lane = lax.broadcasted_iota(jnp.int32, mine.shape, 1)
    tile = jnp.zeros(mine.shape, jnp.float32)
    for k in range(count // mine.shape[0]):
        tile = jnp.where(lane == k, sums[k * mine.shape[0] : (k + 1) * mine.shape[0]], tile)
    mine[...] = tile
    pl.semaphore_wait(barrier, devices - 1)
    copies = [
        pltpu.make_async_remote_copy(
            src_ref=mine,
            dst_ref=others.at[k],
            send_sem=send_sem.at[k],
            recv_sem=recv_sem.at[k],
            device_id=peer,
            device_id_type=MESH,
        )
        for k, peer in enumerate(ahead)
    ]
    for copy in copies:
        copy.start()
    for k, copy in enumerate(copies):
        copy.wait_recv()
        tile = tile + others[k]
    sum_ref[...] = tile
    for copy in copies:
        copy.wait_send()


def close(weights, values, part, inverse):
    count, width = part.shape
    key_heads, rows, span = weights.shape
    head = values.shape[1]
    peers = lax.axis_size("tp") - 1
    vmem = pl.BlockSpec(memory_space=pltpu.VMEM)
    return pl.pallas_call(
        close_kernel,
        in_specs=[vmem] * 4,
        out_specs=[vmem] * 2,
        out_shape=[
            jax.ShapeDtypeStruct((count, width), jnp.float32),
            jax.ShapeDtypeStruct((8, head), jnp.float32),
        ],
        scratch_shapes=[
            pltpu.VMEM((8, head), jnp.float32),
            pltpu.VMEM((peers, 8, head), jnp.float32),
            pltpu.SemaphoreType.DMA((peers,)),
            pltpu.SemaphoreType.DMA((peers,)),
        ],
        compiler_params=pltpu.CompilerParams(
            collective_id=0, has_side_effects=True, vmem_limit_bytes=40 * 2**20
        ),
        cost_estimate=pl.CostEstimate(
            flops=4 * key_heads * rows * span * head, bytes_accessed=4 * 2**20, transcendentals=0
        ),
        name="close",
    )(weights, values, part, inverse)


def write_kernel(
    width, hid_ref, sum_ref, gain_ref, s_ref, t_ref, hv_in, out_ref, hv_ref, buffer, sems
):
    del hv_in
    ends = hv_ref.shape[0]
    moves = []
    for v_ref in (t_ref, s_ref):
        ends -= v_ref.shape[0]
        moves.append(
            pltpu.make_async_copy(v_ref, hv_ref.at[pl.ds(ends, v_ref.shape[0])], sems.at[len(moves)])
        )
        moves[-1].start()
    scale = lax.rsqrt(sum_ref[...] / width + epsilon)
    tall = scale.shape[0]
    step = 2 * tall
    for start in range(0, hid_ref.shape[0], step):
        rows = slice(start, start + step)
        first = start // tall
        each = jnp.concatenate([scale[:, first + k : first + k + 1] for k in range(2)], axis=0)
        buffer[rows, :] = (hid_ref[rows, :] * each * gain_ref[...]).astype(jnp.bfloat16)
        moves.append(
            pltpu.make_async_copy(
                buffer.at[pl.ds(start, step)], out_ref.at[pl.ds(start, step)], sems.at[len(moves)]
            )
        )
        moves[-1].start()
    for move in moves:
        move.wait()


def write(hidden, sums, gain, values, last_values, handed):
    count, columns = hidden.shape
    vmem = pl.BlockSpec(memory_space=pltpu.VMEM)
    anywhere = pl.BlockSpec(memory_space=pl.ANY)
    return pl.pallas_call(
        functools.partial(write_kernel, columns * lax.axis_size("tp")),
        in_specs=[vmem] * 5 + [anywhere],
        out_specs=[anywhere] * 2,
        out_shape=[
            jax.ShapeDtypeStruct((count, columns), jnp.bfloat16),
            jax.ShapeDtypeStruct(handed.shape, jnp.bfloat16),
        ],
        scratch_shapes=[
            pltpu.VMEM((count, columns), jnp.bfloat16),
            pltpu.SemaphoreType.DMA((2 + count // 16,)),
        ],
        input_output_aliases={5: 1},
        compiler_params=pltpu.CompilerParams(vmem_limit_bytes=40 * 2**20),
        cost_estimate=pl.CostEstimate(
            flops=8 * count * columns, bytes_accessed=2 * 2**20, transcendentals=0
        ),
        name="write",
    )(hidden, sums, gain, values, last_values, handed)


def normed(hidden, partial, gain):
    columns = sum(part.shape[1] for part in hidden)
    width = columns * lax.axis_size("tp")
    squares = lax.psum(jnp.sum(sum(partial), axis=1), "tp")
    inverse = lax.rsqrt(squares[:, None] / width + epsilon)
    out, at = [], 0
    for part in hidden:
        here = gain[at : at + part.shape[1]].astype(jnp.float32)
        out.append((part * inverse * here).astype(jnp.bfloat16))
        at += part.shape[1]
    return jnp.concatenate(out, axis=1)


def local(
    prompt_keys,
    prompt_values,
    span_queries,
    span_keys,
    span_values,
    prefill_residual,
    decode_queries,
    decode_keys,
    decode_values,
    decode_residual,
    cursor,
    norm_gain,
):
    span, heads, head = span_queries.shape[1:]
    past, key_heads = prompt_keys.shape[1:3]
    steps, count = decode_keys.shape[1:3]
    group = heads // key_heads
    flat = lambda a: a.reshape(-1, head)
    first, second = routes(lax.axis_size("pair"))
    half_way, far = [], []
    for name, piece in zip(FIRST, (prompt_keys, span_keys, prompt_values, span_values)):
        if name in CROSS:
            half_way.append(crossed(flat(piece), first))
        else:
            half_way.append(lax.ppermute(flat(piece), "pair", first))
    keys = jnp.concatenate([prompt_keys[0], span_keys[0]], axis=0).transpose(1, 0, 2)
    values = jnp.concatenate([prompt_values[0], span_values[0]], axis=0).transpose(1, 0, 2)
    queries = span_queries[0].transpose(1, 0, 2)
    hidden, partial = [], []
    cuts = (0, heads // 2, heads)
    for start, stop in zip(cuts, cuts[1:]):
        done = prefill(queries, keys, values, prefill_residual[0], start, stop)
        hidden.append(done[0])
        partial.append(done[1])
    partial[-1], later = lax.optimization_barrier((partial[-1], half_way[-1]))
    early = span // 2 * key_heads
    far = []
    for name, piece in zip(SECOND, half_way[:-1] + [later[:early], later[early:]]):
        if name in CROSS:
            far.append(crossed(piece, second))
        else:
            far.append(lax.ppermute(piece, "pair", second))
    far_pk, far_sk, far_pv, far_sv, far_tv = far
    prefill_out = normed(hidden, partial, norm_gain)

    dq = decode_queries[0].reshape(steps * count, heads, head).transpose(1, 0, 2)
    dq = dq.reshape(key_heads, group * steps * count, head)
    dk = decode_keys[0].transpose(2, 0, 1, 3)
    dv = decode_values[0].transpose(2, 0, 1, 3)
    block = steps * count * (2 if group % 2 == 0 else 1)
    reach = jnp.tile(cursor[0], block // count)[:, None]
    prefill_out, dq, dk, dv, reach = lax.optimization_barrier((prefill_out, dq, dk, dv, reach))
    weights, ending, inverse, own, handed_keys = weigh(
        dq, far_pk, far_sk, dk, dv, reach, far_tv.shape[0]
    )
    acc, handed = mix(weights, far_pv, own, (past + span) * key_heads)
    residual = decode_residual[0].reshape(steps * count, heads * head)
    part = gather(weights, far_sv, acc, inverse, residual)
    decode_hidden, sums = close(ending, far_tv, part, inverse)
    gain = norm_gain.astype(jnp.float32)[None, :]
    decode_out, handed_values = write(decode_hidden, sums, gain, far_sv, far_tv, handed)
    shape = (1, past + span, key_heads, head)
    return (
        prefill_out[None],
        handed_keys.reshape(shape),
        handed_values.reshape(shape),
        decode_out.reshape(decode_residual.shape),
    )


def solution(mesh):
    row = ("groups", "pair")
    placed = (
        P(row, None, "tp", None),
        P(row, None, "tp", None),
        P(row, None, "tp", None),
        P(row, None, "tp", None),
        P(row, None, "tp", None),
        P(row, None, "tp"),
        P(row, None, None, "tp", None),
        P(row, None, None, "tp", None),
        P(row, None, None, "tp", None),
        P(row, None, None, "tp"),
        P(row, None),
        P("tp"),
    )
    return jax.shard_map(
        local,
        mesh=mesh,
        in_specs=placed,
        out_specs=(
            P(row, None, "tp"),
            P(row, None, "tp", None),
            P(row, None, "tp", None),
            P(row, None, None, "tp"),
        ),
        check_vma=False,
    )
```

profile of v0, /device:TPU:17, one launch (start us, length us, event | category | flops | bytes accessed | tf_op | source)
XLA Modules:
  0.0 117.9 jit_solution(16715693834268445829)
XLA Ops:
  0.7 0.1 collective-permute-start
  0.7 1.9 %collective-permute-start.1 = (bf16[3072,128]{1,0:T(8,128)(2,1)}, bf16[3072,128]{1,0:T(8,128)(2,1)}, u32[]{:S(2)}, u32[]{:S(2)}) collective-permute-start(bf16[3072,128]{1,0:T(8,128)(2,1)} %bitcast.58), channel_id=1, source_target_pairs={{0,4},{4,12},{8,0},{12,8},{1,5},{5,13},{9,1},{13,9},{2,6},{6,14},{... | collective-permute-start | bytes 2359304 | tf_op jit(solution)/shard_map/ppermute | solution.py:433
  2.6 2.3 %collective-permute-start.3 = (bf16[1024,128]{1,0:T(8,128)(2,1)}, bf16[1024,128]{1,0:T(8,128)(2,1)}, u32[]{:S(2)}, u32[]{:S(2)}) collective-permute-start(bf16[1024,128]{1,0:T(8,128)(2,1)} %bitcast.62), channel_id=1, source_target_pairs={{0,4},{4,12},{8,0},{12,8},{1,5},{5,13},{9,1},{13,9},{2,6},{6,14},{... | collective-permute-start | bytes 786440 | tf_op jit(solution)/shard_map/ppermute | solution.py:433
  4.9 0.6 collective-permute-start.7
  5.6 1.0 copy.37
  6.6 1.2 %copy.35 = bf16[1,1536,2,128]{3,1,2,0:T(8,128)(2,1)S(1)} copy(bf16[1,1536,2,128]{3,2,1,0:T(2,128)(2,1)} %param.12) | data formatting | bytes 1572864 | tf_op args[0]
  7.9 0.0 copy-done.4
  7.9 0.1 copy.34
  8.0 0.5 copy.33
  8.5 0.0 copy-start.2
  8.6 0.1 maximum_bitcast_fusion.k_ref
  8.6 0.1 maximum_bitcast_fusion.1.v_ref
  8.7 1.4 %copy-done.2 = bf16[1,512,2048]{2,1,0:T(8,128)(2,1)S(1)} copy-done((bf16[1,512,2048]{2,1,0:T(8,128)(2,1)S(1)}, bf16[1,512,2048]{2,1,0:T(8,128)(2,1)}, u32[]{:S(2)}) %copy-start.2) | copy-done | bytes 2097176
  10.1 16.2 %prefill.2 = (f32[512,1024]{1,0:T(8,128)S(1)}, f32[512,128]{1,0:T(8,128)S(1)}) custom-call(bf16[16,512,128]{2,1,0:T(8,128)(2,1)S(1)} %bitcast.45, bf16[2,2048,128]{2,1,0:T(8,128)(2,1)S(1)} %maximum_bitcast_fusion.k_ref, bf16[2,2048,128]{2,1,0:T(8,128)(2,1)S(1)} %maximum_bitcast_fusion.1.v_ref, bf16[512,2048]{1,0:T(8,128)(2,1)S(1)} %bitcast.50), custom_call_target="tpu_custom_call" | custom-call | flops 8589934592 | bytes 8388608 | tf_op jit(solution)/shard_map/prefill/pallas_call | solution.py:73
  26.3 0.0 copy-start.9
  26.3 0.0 copy-start.5
  26.4 0.0 copy-start.10
  26.4 0.0 copy-start.7
  26.4 0.0 copy-start.8
  26.4 16.2 %prefill.3 = (f32[512,1024]{1,0:T(8,128)S(1)}, f32[512,128]{1,0:T(8,128)S(1)}) custom-call(bf16[16,512,128]{2,1,0:T(8,128)(2,1)S(1)} %bitcast.46, bf16[2,2048,128]{2,1,0:T(8,128)(2,1)S(1)} %maximum_bitcast_fusion.k_ref, bf16[2,2048,128]{2,1,0:T(8,128)(2,1)S(1)} %maximum_bitcast_fusion.1.v_ref, bf16[512,2048]{1,0:T(8,128)(2,1)S(1)} %bitcast.51), custom_call_target="tpu_custom_call" | custom-call | flops 8589934592 | bytes 8388608 | tf_op jit(solution)/shard_map/prefill/pallas_call | solution.py:73
  42.6 0.0 copy-start
  42.6 1.3 %copy-done = f32[512,1024]{1,0:T(8,128)} copy-done((f32[512,1024]{1,0:T(8,128)}, f32[512,1024]{1,0:T(8,128)S(1)}, u32[]{:S(2)}) %copy-start) | copy-done | bytes 2097176
  43.9 0.1 copy.22
  44.0 0.1 broadcast_in_dim_tile.3
  44.1 0.0 collective-permute-done
  44.2 0.1 add_reduce_fusion
  44.3 5.5 %psum.7 = f32[512]{0:T(512)S(1)} all-reduce(f32[512]{0:T(512)S(1)} %add_reduce_fusion), channel_id=1, replica_groups=mesh['groups'=2,'pair'=4,'tp'=4] {'tp'}, use_global_device_ids=true, to_apply=%region_1.0 | all-reduce | flops 512 | bytes 4096 | tf_op jit(solution)/shard_map/psum | solution.py:398
  49.8 0.0 collective-permute-done.1
  49.8 1.9 %collective-permute-start.2 = (bf16[3072,128]{1,0:T(8,128)(2,1)}, bf16[3072,128]{1,0:T(8,128)(2,1)}, u32[]{:S(2)}, u32[]{:S(2)}) collective-permute-start(bf16[3072,128]{1,0:T(8,128)(2,1)} %collective-permute-done.1), channel_id=1, source_target_pairs={{0,0},{4,8},{8,4},{12,12},{1,1},{5,9},{9,5},{13,13},{2,2},{6,10},{... | collective-permute-start | bytes 2359304 | tf_op jit(solution)/shard_map/ppermute | solution.py:450
  51.8 0.0 collective-permute-done.7
  51.8 3.8 %collective-permute-start.8 = (bf16[3072,128]{1,0:T(8,128)(2,1)}, bf16[3072,128]{1,0:T(8,128)(2,1)S(1)}, u32[]{:S(2)}, u32[]{:S(2)}) collective-permute-start(bf16[3072,128]{1,0:T(8,128)(2,1)} %collective-permute-done.7), channel_id=1, source_target_pairs={{0,1},{1,0},{2,3},{3,2},{4,9},{5,8},{6,11},{7,10},{8,5},{9,4},{10,... | collective-permute-start | bytes 2359304 | tf_op jit(solution)/shard_map/ppermute | solution.py:37
  55.6 2.0 %multiply_convert_fusion.1 = (bf16[512,1024]{1,0:T(8,128)(2,1)S(1)}, bf16[512,1024]{1,0:T(8,128)(2,1)S(1)}) fusion(f32[512,1024]{1,0:T(8,128)S(1)} %get-tuple-element.26, f32[1024]{0:T(1024)S(1)} %get-tuple-element.50, f32[512]{0:T(512)S(1)} %add_rsqrt_fusion, f32[1024]{0:T(1024)S(1)} %get-tuple-element.51, f32[512,1024]{1,0:T(8,128)} %copy-done), kind=kLoop, calls=%fused_computation.3 | loop fusion | flops 3145728 | bytes 6301696 | tf_op jit(solution)/shard_map/convert_element_type | solution.py:403
  57.6 0.0 collective-permute-done.3
  57.7 1.9 %collective-permute-start.4 = (bf16[1024,128]{1,0:T(8,128)(2,1)}, bf16[1024,128]{1,0:T(8,128)(2,1)S(1)}, u32[]{:S(2)}, u32[]{:S(2)}) collective-permute-start(bf16[1024,128]{1,0:T(8,128)(2,1)} %collective-permute-done.3), channel_id=1, source_target_pairs={{0,0},{4,8},{8,4},{12,12},{1,1},{5,9},{9,5},{13,13},{2,2},{6,10},{... | collective-permute-start | bytes 786440 | tf_op jit(solution)/shard_map/ppermute | solution.py:450
  59.6 1.5 %pad_maximum_fusion = bf16[512,2048]{1,0:T(8,128)(2,1)} fusion(bf16[512,1024]{1,0:T(8,128)(2,1)S(1)} %get-tuple-element.53, bf16[512,1024]{1,0:T(8,128)(2,1)S(1)} %get-tuple-element.52), kind=kLoop, calls=%fused_computation | loop fusion | flops 4194304 | bytes 4194304 | tf_op jit(solution)/shard_map/concatenate | solution.py:405
  61.1 0.1 copy.25.cur_ref
  61.2 0.3 collective-permute-start.5
  61.5 1.5 %collective-permute-start.6 = (bf16[512,128]{1,0:T(8,128)(2,1)S(1)}, bf16[512,128]{1,0:T(8,128)(2,1)S(1)}, u32[]{:S(2)}, u32[]{:S(2)}) collective-permute-start(bf16[512,128]{1,0:T(8,128)(2,1)S(1)} %get-tuple-element.48), channel_id=1, source_target_pairs={{0,1},{1,0},{2,3},{3,2},{4,9},{5,8},{6,11},{7,10},{8,5},{9,4},{10,... | collective-permute-start | bytes 393224 | tf_op jit(solution)/shard_map/ppermute | solution.py:37
  63.0 28.3 %collective-permute-done.4.sk_ref = bf16[1024,128]{1,0:T(8,128)(2,1)S(1)} collective-permute-done((bf16[1024,128]{1,0:T(8,128)(2,1)}, bf16[1024,128]{1,0:T(8,128)(2,1)S(1)}, u32[]{:S(2)}, u32[]{:S(2)}) %collective-permute-start.4) | collective-permute-done | bytes 262176 | tf_op jit(solution)/shard_map/ppermute | solution.py:450
  91.4 0.0 collective-permute-done.2.pk_ref
  91.4 12.7 %weigh.1 = (bf16[2,512,3584]{2,1,0:T(8,128)(2,1)S(1)}, bf16[2,512,512]{2,1,0:T(8,128)(2,1)S(1)}, f32[2,512,128]{2,1,0:T(8,128)S(1)}, f32[2,512,128]{2,1,0:T(8,128)S(1)}, bf16[4096,128]{1,0:T(8,128)(2,1)}) custom-call(bf16[2,512,128]{2,1,0:T(8,128)(2,1)S(1)} %bitcast.48, bf16[3072,128]{1,0:T(8,128)(2,1)} %collective-permute-done.2.pk_ref, ...), custom_call_target="tpu_custom_call" | custom-call | flops 2147483648 | bytes 16777216 | tf_op jit(solution)/shard_map/weigh/pallas_call | solution.py:157
  104.0 0.0 collective-permute-done.8.v_ref
  104.0 3.2 %mix.1 = (f32[2,512,128]{2,1,0:T(8,128)S(1)}, bf16[4096,128]{1,0:T(8,128)(2,1)}) custom-call(bf16[2,512,3584]{2,1,0:T(8,128)(2,1)S(1)} %get-tuple-element.39.w_ref, bf16[3072,128]{1,0:T(8,128)(2,1)S(1)} %collective-permute-done.8.v_ref, f32[2,512,128]{2,1,0:T(8,128)S(1)} %get-tuple-element.40.own_ref), custom_call_target="tpu_custom_call" | custom-call | flops 1610612736 | bytes 8388608 | tf_op jit(solution)/shard_map/mix/pallas_call | solution.py:203
  107.2 0.0 collective-permute-done.6.v_ref.s_ref
  107.2 0.8 gather.1.part_ref
  108.0 0.0 collective-permute-done.5.v_ref.t_ref
  108.0 8.9 %close.1 = (f32[64,2048]{1,0:T(8,128)S(1)}, f32[8,128]{1,0:T(8,128)S(1)}) custom-call(bf16[2,512,512]{2,1,0:T(8,128)(2,1)S(1)} %get-tuple-element.37.w_ref, bf16[512,128]{1,0:T(8,128)(2,1)S(1)} %collective-permute-done.5.v_ref.t_ref, f32[64,2048]{1,0:T(8,128)S(1)} %gather.1.part_ref, f32[2,512,128]{2,1,0:T(8,128)S(1)} %get-tuple-element.42.inv_ref), custom_call_target="tpu_custom_call" | custom-call | flops 268435456 | bytes 4194304 | tf_op jit(solution)/shard_map/close/pallas_call | solution.py:316
  117.0 0.9 write.1
  (19 shorter events, 0.1 us)
Async XLA Ops:
  0.6 7.2 %copy-start.6 = (bf16[1,512,2,128]{3,2,1,0:T(2,128)(2,1)S(1)}, bf16[1,512,2,128]{3,2,1,0:T(2,128)(2,1)}, u32[]{:S(2)}) copy-start(bf16[1,512,2,128]{3,2,1,0:T(2,128)(2,1)} %param.16) | copy-start | bytes 786436
  0.6 7.2 %copy-start.4 = (bf16[1,1536,2,128]{3,2,1,0:T(2,128)(2,1)S(1)}, bf16[1,1536,2,128]{3,2,1,0:T(2,128)(2,1)}, u32[]{:S(2)}) copy-start(bf16[1,1536,2,128]{3,2,1,0:T(2,128)(2,1)} %param.13) | copy-start | bytes 2359300
  0.7 43.5 %collective-permute-start = (bf16[1024,128]{1,0:T(8,128)(2,1)}, bf16[1024,128]{1,0:T(8,128)(2,1)S(1)}, u32[]{:S(2)}, u32[]{:S(2)}) collective-permute-start(bf16[1024,128]{1,0:T(8,128)(2,1)} %bitcast.61), channel_id=1, source_target_pairs={{0,5},{1,4},{2,7},{3,6},{4,13},{5,12},{6,15},{7,14},{8,1},{9,0},{1... | collective-permute-start | bytes 786440 | tf_op jit(solution)/shard_map/ppermute | solution.py:37
  0.7 49.1 %collective-permute-start.1 = (bf16[3072,128]{1,0:T(8,128)(2,1)}, bf16[3072,128]{1,0:T(8,128)(2,1)}, u32[]{:S(2)}, u32[]{:S(2)}) collective-permute-start(bf16[3072,128]{1,0:T(8,128)(2,1)} %bitcast.58), channel_id=1, source_target_pairs={{0,4},{4,12},{8,0},{12,8},{1,5},{5,13},{9,1},{13,9},{2,6},{6,14},{... | collective-permute-start | bytes 2359304 | tf_op jit(solution)/shard_map/ppermute | solution.py:433
  2.6 55.0 %collective-permute-start.3 = (bf16[1024,128]{1,0:T(8,128)(2,1)}, bf16[1024,128]{1,0:T(8,128)(2,1)}, u32[]{:S(2)}, u32[]{:S(2)}) collective-permute-start(bf16[1024,128]{1,0:T(8,128)(2,1)} %bitcast.62), channel_id=1, source_target_pairs={{0,4},{4,12},{8,0},{12,8},{1,5},{5,13},{9,1},{13,9},{2,6},{6,14},{... | collective-permute-start | bytes 786440 | tf_op jit(solution)/shard_map/ppermute | solution.py:433
  4.9 3.1 %copy-start.3 = (bf16[1,512,16,128]{3,2,1,0:T(8,128)(2,1)S(1)}, bf16[1,512,16,128]{3,2,1,0:T(8,128)(2,1)}, u32[]{:S(2)}) copy-start(bf16[1,512,16,128]{3,2,1,0:T(8,128)(2,1)} %param.14) | copy-start | bytes 6291460
  4.9 46.8 %collective-permute-start.7 = (bf16[3072,128]{1,0:T(8,128)(2,1)}, bf16[3072,128]{1,0:T(8,128)(2,1)}, u32[]{:S(2)}, u32[]{:S(2)}) collective-permute-start(bf16[3072,128]{1,0:T(8,128)(2,1)} %bitcast.59), channel_id=1, source_target_pairs={{0,5},{1,4},{2,7},{3,6},{4,13},{5,12},{6,15},{7,14},{8,1},{9,0},{1... | collective-permute-start | bytes 2359304 | tf_op jit(solution)/shard_map/ppermute | solution.py:37
  8.5 1.6 %copy-start.2 = (bf16[1,512,2048]{2,1,0:T(8,128)(2,1)S(1)}, bf16[1,512,2048]{2,1,0:T(8,128)(2,1)}, u32[]{:S(2)}) copy-start(bf16[1,512,2048]{2,1,0:T(8,128)(2,1)} %param.17) | copy-start | bytes 6291460
  26.3 17.6 %copy-start.9 = (bf16[2048]{0:T(1024)(128)(2,1)S(1)}, bf16[2048]{0:T(1024)(128)(2,1)}, u32[]{:S(2)}) copy-start(bf16[2048]{0:T(1024)(128)(2,1)} %param.23) | copy-start | bytes 12292
  26.3 17.6 %copy-start.5 = (bf16[1,2,32,16,128]{4,3,2,1,0:T(8,128)(2,1)S(1)}, bf16[1,2,32,16,128]{4,3,2,1,0:T(8,128)(2,1)}, u32[]{:S(2)}) copy-start(bf16[1,2,32,16,128]{4,3,2,1,0:T(8,128)(2,1)} %param.18) | copy-start | bytes 786436
  26.4 17.7 %copy-start.10 = (s32[1,32]{1,0:T(1,128)S(1)}, s32[1,32]{1,0:T(1,128)}, u32[]{:S(2)}) copy-start(s32[1,32]{1,0:T(1,128)} %param.22) | copy-start | bytes 388
  26.4 17.8 %copy-start.7 = (bf16[1,2,32,2,128]{4,3,2,1,0:T(2,128)(2,1)S(1)}, bf16[1,2,32,2,128]{4,3,2,1,0:T(2,128)(2,1)}, u32[]{:S(2)}) copy-start(bf16[1,2,32,2,128]{4,3,2,1,0:T(2,128)(2,1)} %param.20) | copy-start | bytes 98308
  26.4 17.8 %copy-start.8 = (bf16[1,2,32,2,128]{4,3,2,1,0:T(2,128)(2,1)S(1)}, bf16[1,2,32,2,128]{4,3,2,1,0:T(2,128)(2,1)}, u32[]{:S(2)}) copy-start(bf16[1,2,32,2,128]{4,3,2,1,0:T(2,128)(2,1)} %param.19) | copy-start | bytes 98308
  42.6 1.3 %copy-start = (f32[512,1024]{1,0:T(8,128)}, f32[512,1024]{1,0:T(8,128)S(1)}, u32[]{:S(2)}) copy-start(f32[512,1024]{1,0:T(8,128)S(1)} %get-tuple-element.30) | copy-start | bytes 6291460
  49.8 41.5 %collective-permute-start.2 = (bf16[3072,128]{1,0:T(8,128)(2,1)}, bf16[3072,128]{1,0:T(8,128)(2,1)}, u32[]{:S(2)}, u32[]{:S(2)}) collective-permute-start(bf16[3072,128]{1,0:T(8,128)(2,1)} %collective-permute-done.1), channel_id=1, source_target_pairs={{0,0},{4,8},{8,4},{12,12},{1,1},{5,9},{9,5},{13,13},{2,2},{6,10},{... | collective-permute-start | bytes 2359304 | tf_op jit(solution)/shard_map/ppermute | solution.py:450
  51.8 52.2 %collective-permute-start.8 = (bf16[3072,128]{1,0:T(8,128)(2,1)}, bf16[3072,128]{1,0:T(8,128)(2,1)S(1)}, u32[]{:S(2)}, u32[]{:S(2)}) collective-permute-start(bf16[3072,128]{1,0:T(8,128)(2,1)} %collective-permute-done.7), channel_id=1, source_target_pairs={{0,1},{1,0},{2,3},{3,2},{4,9},{5,8},{6,11},{7,10},{8,5},{9,4},{10,... | collective-permute-start | bytes 2359304 | tf_op jit(solution)/shard_map/ppermute | solution.py:37
  57.7 33.7 %collective-permute-start.4 = (bf16[1024,128]{1,0:T(8,128)(2,1)}, bf16[1024,128]{1,0:T(8,128)(2,1)S(1)}, u32[]{:S(2)}, u32[]{:S(2)}) collective-permute-start(bf16[1024,128]{1,0:T(8,128)(2,1)} %collective-permute-done.3), channel_id=1, source_target_pairs={{0,0},{4,8},{8,4},{12,12},{1,1},{5,9},{9,5},{13,13},{2,2},{6,10},{... | collective-permute-start | bytes 786440 | tf_op jit(solution)/shard_map/ppermute | solution.py:450
  61.2 46.8 %collective-permute-start.5 = (bf16[512,128]{1,0:T(8,128)(2,1)S(1)}, bf16[512,128]{1,0:T(8,128)(2,1)S(1)}, u32[]{:S(2)}, u32[]{:S(2)}) collective-permute-start(bf16[512,128]{1,0:T(8,128)(2,1)S(1)} %get-tuple-element.49), channel_id=1, source_target_pairs={{0,1},{1,0},{2,3},{3,2},{4,9},{5,8},{6,11},{7,10},{8,5},{9,4},{10,... | collective-permute-start | bytes 393224 | tf_op jit(solution)/shard_map/ppermute | solution.py:37
  61.5 45.7 %collective-permute-start.6 = (bf16[512,128]{1,0:T(8,128)(2,1)S(1)}, bf16[512,128]{1,0:T(8,128)(2,1)S(1)}, u32[]{:S(2)}, u32[]{:S(2)}) collective-permute-start(bf16[512,128]{1,0:T(8,128)(2,1)S(1)} %get-tuple-element.48), channel_id=1, source_target_pairs={{0,1},{1,0},{2,3},{3,2},{4,9},{5,8},{6,11},{7,10},{8,5},{9,4},{10,... | collective-permute-start | bytes 393224 | tf_op jit(solution)/shard_map/ppermute | solution.py:37
  104.0 3.2 %copy-start.1 = (bf16[1,2,32,2048]{3,2,1,0:T(8,128)(2,1)S(1)}, bf16[1,2,32,2048]{3,2,1,0:T(8,128)(2,1)}, u32[]{:S(2)}) copy-start(bf16[1,2,32,2048]{3,2,1,0:T(8,128)(2,1)} %param.21) | copy-start | bytes 786436
where the time goes:
time: 119 us; the launch traced here: 118 us
  Pallas kernels  58.8 us (49%)
  waiting for transfers between devices  28.3 us (24%)
  starting transfers between devices  14.4 us (12%)
  local copies, waits for them, and re-layouts  6.02 us (5%)
  blocking collectives  5.52 us (5%)
  other arithmetic  3.84 us (3%)
    pallas_call x2, Pallas kernels, prefill(): pl.pallas_call(functools.partial(prefill_kernel, block, positions - span,...  32.4 us
    ppermute x2, waiting for transfers between devices, local(): far.append(lax.ppermute(piece, 'pair', second))  28.3 us
    pallas_call x1, Pallas kernels, weigh(): pl.pallas_call(functools.partial(weigh_kernel, head ** (-0.5), key_heads,...  12.7 us
    pallas_call x1, Pallas kernels, close(): pl.pallas_call(close_kernel, in_specs=[vmem] * 4, out_specs=[vmem] * 2, o...  8.93 us
    ppermute x5, starting transfers between devices, crossed(): return lax.ppermute(value, ('pair', 'tp'), both)  6.32 us
    unnamed x27, local copies, waits for them, and re-layouts  5.73 us
    psum x1, blocking collectives, normed(): squares = lax.psum(jnp.sum(sum(partial), axis=1), 'tp')  5.52 us
    ppermute x2, starting transfers between devices, local(): half_way.append(lax.ppermute(flat(piece), 'pair', first))  4.21 us
  transfers between devices with their start and end apart: 9, of which 1 were waited for; matrix products, arithmetic and copies ran while one was open for 6% of the time, Pallas kernels for 42%

commit v1 on v0

--- a/solution.py
+++ b/solution.py
@@ -10,7 +10,7 @@
 
 epsilon = 1e-05
 FIRST = ("half_pk", "half_sk", "half_pv", "half_sv")
-SECOND = ("full_pk", "full_sk", "full_pv", "full_sv", "full_tv")
+SECOND = ("full_pk", "full_sk", "full_pv", "full_sv")
 CROSS = FIRST[2:] + SECOND[2:]
 NT = (((1,), (1,)), ((), ()))
 MESH = pl.DeviceIdType.MESH
@@ -189,17 +189,24 @@
     )(queries, prompt_keys, span_keys, own_keys, own_values, reach)
 
 
-def mix_kernel(w_ref, v_ref, own_ref, acc_ref, hv_ref):
+def mix_kernel(w_ref, v_ref, own_ref, inv_ref, res_ref, part_ref, hv_ref):
     @pl.when(pl.program_id(0) == 0)
     def _():
         hv_ref[...] = v_ref[...]
 
-    acc_ref[0] = own_ref[0] + jnp.dot(w_ref[0], v_ref[...], preferred_element_type=jnp.float32)
-
-
-def mix(weights, prompt_values, own, both):
+    mixed = own_ref[0] + jnp.dot(w_ref[0], v_ref[...], preferred_element_type=jnp.float32)
+    mixed = mixed * inv_ref[0]
+    count = res_ref.shape[0]
+    head = mixed.shape[1]
+    for h in range(mixed.shape[0] // count):
+        columns = slice(h * head, (h + 1) * head)
+        part_ref[:, columns] = mixed[h * count : (h + 1) * count] + res_ref[:, columns].astype(jnp.float32)
+
+
+def mix(weights, prompt_values, own, inverse, residual, both):
     key_heads, rows, _ = weights.shape
     past, head = prompt_values.shape
+    count, width = residual.shape
     return pl.pallas_call(
         mix_kernel,
         grid=(key_heads,),
@@ -207,13 +214,15 @@
             pl.BlockSpec((1, rows, past), lambda g: (g, 0, 0)),
             pl.BlockSpec((past, head), lambda g: (0, 0)),
             pl.BlockSpec((1, rows, head), lambda g: (g, 0, 0)),
+            pl.BlockSpec((1, rows, head), lambda g: (g, 0, 0)),
+            pl.BlockSpec((count, width // key_heads), lambda g: (0, g)),
         ],
         out_specs=[
-            pl.BlockSpec((1, rows, head), lambda g: (g, 0, 0)),
+            pl.BlockSpec((count, width // key_heads), lambda g: (0, g)),
             pl.BlockSpec((past, head), lambda g: (0, 0)),
         ],
         out_shape=[
-            jax.ShapeDtypeStruct((key_heads, rows, head), jnp.float32),
+            jax.ShapeDtypeStruct((count, width), jnp.float32),
             jax.ShapeDtypeStruct((both, head), jnp.bfloat16),
         ],
         compiler_params=pltpu.CompilerParams(vmem_limit_bytes=40 * 2**20),
@@ -221,42 +230,7 @@
             flops=4 * key_heads * rows * past * head, bytes_accessed=8 * 2**20, transcendentals=0
         ),
         name="mix",
-    )(weights, prompt_values, own)
-
-
-def gather_kernel(w_ref, v_ref, acc_ref, inv_ref, res_ref, part_ref):
-    mixed = acc_ref[0] + jnp.dot(w_ref[0], v_ref[...], preferred_element_type=jnp.float32)
-    mixed = mixed * inv_ref[0]
-    count = res_ref.shape[0]
-    head = mixed.shape[1]
-    for h in range(mixed.shape[0] // count):
-        columns = slice(h * head, (h + 1) * head)
-        part_ref[:, columns] = mixed[h * count : (h + 1) * count] + res_ref[:, columns].astype(jnp.float32)
-
-
-def gather(weights, span_values, acc, inverse, residual):
-    key_heads, rows, columns = weights.shape
-    span, head = span_values.shape
-    count, width = residual.shape
-    at = columns // span - 1
-    return pl.pallas_call(
-        gather_kernel,
-        grid=(key_heads,),
-        in_specs=[
-            pl.BlockSpec((1, rows, span), lambda g: (g, 0, at)),
-            pl.BlockSpec((span, head), lambda g: (0, 0)),
-            pl.BlockSpec((1, rows, head), lambda g: (g, 0, 0)),
-            pl.BlockSpec((1, rows, head), lambda g: (g, 0, 0)),
-            pl.BlockSpec((count, width // key_heads), lambda g: (0, g)),
-        ],
-        out_specs=pl.BlockSpec((count, width // key_heads), lambda g: (0, g)),
-        out_shape=jax.ShapeDtypeStruct((count, width), jnp.float32),
-        compiler_params=pltpu.CompilerParams(vmem_limit_bytes=40 * 2**20),
-        cost_estimate=pl.CostEstimate(
-            flops=4 * key_heads * rows * span * head, bytes_accessed=6 * 2**20, transcendentals=0
-        ),
-        name="gather",
-    )(weights, span_values, acc, inverse, residual)
+    )(weights, prompt_values, own, inverse, residual)
 
 
 def close_kernel(
@@ -338,12 +312,12 @@
 
 
 def write_kernel(
-    width, hid_ref, sum_ref, gain_ref, s_ref, t_ref, hv_in, out_ref, hv_ref, buffer, sems
+    width, hid_ref, sum_ref, gain_ref, s_ref, hv_in, out_ref, hv_ref, buffer, sems
 ):
     del hv_in
     ends = hv_ref.shape[0]
     moves = []
-    for v_ref in (t_ref, s_ref):
+    for v_ref in (s_ref,):
         ends -= v_ref.shape[0]
         moves.append(
             pltpu.make_async_copy(v_ref, hv_ref.at[pl.ds(ends, v_ref.shape[0])], sems.at[len(moves)])
@@ -367,13 +341,13 @@
         move.wait()
 
 
-def write(hidden, sums, gain, values, last_values, handed):
+def write(hidden, sums, gain, values, handed):
     count, columns = hidden.shape
     vmem = pl.BlockSpec(memory_space=pltpu.VMEM)
     anywhere = pl.BlockSpec(memory_space=pl.ANY)
     return pl.pallas_call(
         functools.partial(write_kernel, columns * lax.axis_size("tp")),
-        in_specs=[vmem] * 5 + [anywhere],
+        in_specs=[vmem] * 4 + [anywhere],
         out_specs=[anywhere] * 2,
         out_shape=[
             jax.ShapeDtypeStruct((count, columns), jnp.bfloat16),
@@ -383,13 +357,13 @@
             pltpu.VMEM((count, columns), jnp.bfloat16),
             pltpu.SemaphoreType.DMA((2 + count // 16,)),
         ],
-        input_output_aliases={5: 1},
+        input_output_aliases={4: 1},
         compiler_params=pltpu.CompilerParams(vmem_limit_bytes=40 * 2**20),
         cost_estimate=pl.CostEstimate(
             flops=8 * count * columns, bytes_accessed=2 * 2**20, transcendentals=0
         ),
         name="write",
-    )(hidden, sums, gain, values, last_values, handed)
+    )(hidden, sums, gain, values, handed)
 
 
 def normed(hidden, partial, gain):
@@ -441,14 +415,13 @@
         hidden.append(done[0])
         partial.append(done[1])
     partial[-1], later = lax.optimization_barrier((partial[-1], half_way[-1]))
-    early = span // 2 * key_heads
     far = []
-    for name, piece in zip(SECOND, half_way[:-1] + [later[:early], later[early:]]):
+    for name, piece in zip(SECOND, half_way[:-1] + [later]):
         if name in CROSS:
             far.append(crossed(piece, second))
         else:
             far.append(lax.ppermute(piece, "pair", second))
-    far_pk, far_sk, far_pv, far_sv, far_tv = far
+    far_pk, far_sk, far_pv, far_sv = far
     prefill_out = normed(hidden, partial, norm_gain)
 
     dq = decode_queries[0].reshape(steps * count, heads, head).transpose(1, 0, 2)
@@ -459,14 +432,13 @@
     reach = jnp.tile(cursor[0], block // count)[:, None]
     prefill_out, dq, dk, dv, reach = lax.optimization_barrier((prefill_out, dq, dk, dv, reach))
     weights, ending, inverse, own, handed_keys = weigh(
-        dq, far_pk, far_sk, dk, dv, reach, far_tv.shape[0]
+        dq, far_pk, far_sk, dk, dv, reach, far_sv.shape[0]
     )
-    acc, handed = mix(weights, far_pv, own, (past + span) * key_heads)
     residual = decode_residual[0].reshape(steps * count, heads * head)
-    part = gather(weights, far_sv, acc, inverse, residual)
-    decode_hidden, sums = close(ending, far_tv, part, inverse)
+    part, handed = mix(weights, far_pv, own, inverse, residual, (past + span) * key_heads)
+    decode_hidden, sums = close(ending, far_sv, part, inverse)
     gain = norm_gain.astype(jnp.float32)[None, :]
-    decode_out, handed_values = write(decode_hidden, sums, gain, far_sv, far_tv, handed)
+    decode_out, handed_values = write(decode_hidden, sums, gain, far_sv, handed)
     shape = (1, past + span, key_heads, head)
     return (
         prefill_out[None],

time: 119 us -> 103 us (0.87)
  the two profiles are of different devices: /device:TPU:17 before, /device:TPU:9 now
where the time goes in v1:
time: 103 us; the launch traced here: 102 us
  Pallas kernels  52.4 us (51%)
  waiting for transfers between devices  18.8 us (18%)
  starting transfers between devices  13.9 us (13%)
  local copies, waits for them, and re-layouts  6.68 us (6%)
  blocking collectives  5.42 us (5%)
  other arithmetic  3.84 us (4%)
    pallas_call x2, Pallas kernels, prefill(): pl.pallas_call(functools.partial(prefill_kernel, block, positions - span,...  32.4 us
    pallas_call x1, Pallas kernels, weigh(): pl.pallas_call(functools.partial(weigh_kernel, head ** (-0.5), key_heads,...  12.8 us
    ppermute x2, waiting for transfers between devices, local(): far.append(lax.ppermute(piece, 'pair', second))  9.61 us
    ppermute x4, waiting for transfers between devices, crossed(): return lax.ppermute(value, ('pair', 'tp'), both)  9.2 us
    ppermute x4, starting transfers between devices, crossed(): return lax.ppermute(value, ('pair', 'tp'), both)  8.44 us
    unnamed x31, local copies, waits for them, and re-layouts  6.4 us
    psum x1, blocking collectives, normed(): squares = lax.psum(jnp.sum(sum(partial), axis=1), 'tp')  5.42 us
    ppermute x2, starting transfers between devices, local(): far.append(lax.ppermute(piece, 'pair', second))  5.31 us
  transfers between devices with their start and end apart: 8, of which 2 were waited for; matrix products, arithmetic and copies ran while one was open for 7% of the time, Pallas kernels for 47%

profile of v1, /device:TPU:9, one launch (start us, length us, event | category | flops | bytes accessed | tf_op | source)
XLA Modules:
  0.0 102.0 jit_solution(985111680419476634)
XLA Ops:
  0.7 2.9 %collective-permute-start = (bf16[1024,128]{1,0:T(8,128)(2,1)}, bf16[1024,128]{1,0:T(8,128)(2,1)S(1)}, u32[]{:S(2)}, u32[]{:S(2)}) collective-permute-start(bf16[1024,128]{1,0:T(8,128)(2,1)} %bitcast.61), channel_id=1, source_target_pairs={{0,5},{1,4},{2,7},{3,6},{4,13},{5,12},{6,15},{7,14},{8,1},{9,0},{1... | collective-permute-start | bytes 786440 | tf_op jit(solution)/shard_map/ppermute | solution.py:37
  3.6 0.2 collective-permute-start.1
  3.7 0.0 collective-permute-start.3
  3.8 1.6 %collective-permute-start.6 = (bf16[3072,128]{1,0:T(8,128)(2,1)}, bf16[3072,128]{1,0:T(8,128)(2,1)}, u32[]{:S(2)}, u32[]{:S(2)}) collective-permute-start(bf16[3072,128]{1,0:T(8,128)(2,1)} %bitcast.59), channel_id=1, source_target_pairs={{0,5},{1,4},{2,7},{3,6},{4,13},{5,12},{6,15},{7,14},{8,1},{9,0},{1... | collective-permute-start | bytes 2359304 | tf_op jit(solution)/shard_map/ppermute | solution.py:37
  5.4 1.0 copy.37
  6.4 1.2 %copy.35 = bf16[1,1536,2,128]{3,1,2,0:T(8,128)(2,1)S(1)} copy(bf16[1,1536,2,128]{3,2,1,0:T(2,128)(2,1)} %param.12) | data formatting | bytes 1572864 | tf_op args[0]
  7.7 0.1 copy.34
  7.8 0.5 copy.33
  8.3 0.0 copy-start.2
  8.4 0.1 maximum_bitcast_fusion.k_ref
  8.4 0.1 maximum_bitcast_fusion.1.v_ref
  8.5 1.4 %copy-done.2 = bf16[1,512,2048]{2,1,0:T(8,128)(2,1)S(1)} copy-done((bf16[1,512,2048]{2,1,0:T(8,128)(2,1)S(1)}, bf16[1,512,2048]{2,1,0:T(8,128)(2,1)}, u32[]{:S(2)}) %copy-start.2) | copy-done | bytes 2097176
  9.9 16.2 %prefill.2 = (f32[512,1024]{1,0:T(8,128)S(1)}, f32[512,128]{1,0:T(8,128)S(1)}) custom-call(bf16[16,512,128]{2,1,0:T(8,128)(2,1)S(1)} %bitcast.45, bf16[2,2048,128]{2,1,0:T(8,128)(2,1)S(1)} %maximum_bitcast_fusion.k_ref, bf16[2,2048,128]{2,1,0:T(8,128)(2,1)S(1)} %maximum_bitcast_fusion.1.v_ref, bf16[512,2048]{1,0:T(8,128)(2,1)S(1)} %bitcast.50), custom_call_target="tpu_custom_call" | custom-call | flops 8589934592 | bytes 8388608 | tf_op jit(solution)/shard_map/prefill/pallas_call | solution.py:73
  26.1 0.0 copy-start.9
  26.1 0.0 copy-start.5
  26.1 0.0 copy-start.10
  26.2 0.0 copy-start.7
  26.2 0.0 copy-start.8
  26.2 16.2 %prefill.3 = (f32[512,1024]{1,0:T(8,128)S(1)}, f32[512,128]{1,0:T(8,128)S(1)}) custom-call(bf16[16,512,128]{2,1,0:T(8,128)(2,1)S(1)} %bitcast.46, bf16[2,2048,128]{2,1,0:T(8,128)(2,1)S(1)} %maximum_bitcast_fusion.k_ref, bf16[2,2048,128]{2,1,0:T(8,128)(2,1)S(1)} %maximum_bitcast_fusion.1.v_ref, bf16[512,2048]{1,0:T(8,128)(2,1)S(1)} %bitcast.51), custom_call_target="tpu_custom_call" | custom-call | flops 8589934592 | bytes 8388608 | tf_op jit(solution)/shard_map/prefill/pallas_call | solution.py:73
  42.4 0.0 copy-start
  42.4 1.3 %copy-done = f32[512,1024]{1,0:T(8,128)} copy-done((f32[512,1024]{1,0:T(8,128)}, f32[512,1024]{1,0:T(8,128)S(1)}, u32[]{:S(2)}) %copy-start) | copy-done | bytes 2097176
  43.7 0.1 copy.22
  43.8 0.1 broadcast_in_dim_tile.3
  43.9 0.0 collective-permute-done
  44.0 0.0 copy-start.11
  44.0 0.7 copy-done.11
  44.7 0.0 collective-permute-done.3
  44.7 3.4 %collective-permute-start.4 = (bf16[1024,128]{1,0:T(8,128)(2,1)}, bf16[1024,128]{1,0:T(8,128)(2,1)S(1)}, u32[]{:S(2)}, u32[]{:S(2)}) collective-permute-start(bf16[1024,128]{1,0:T(8,128)(2,1)} %collective-permute-done.3), channel_id=1, source_target_pairs={{0,0},{4,8},{8,4},{12,12},{1,1},{5,9},{9,5},{13,13},{2,2},{6,10},{... | collective-permute-start | bytes 786440 | tf_op jit(solution)/shard_map/ppermute | solution.py:423
  48.1 0.1 add_reduce_fusion
  48.2 5.4 %psum.7 = f32[512]{0:T(512)S(1)} all-reduce(f32[512]{0:T(512)S(1)} %add_reduce_fusion), channel_id=1, replica_groups=mesh['groups'=2,'pair'=4,'tp'=4] {'tp'}, use_global_device_ids=true, to_apply=%region_1.0 | all-reduce | flops 512 | bytes 4096 | tf_op jit(solution)/shard_map/psum | solution.py:372
  53.6 0.0 collective-permute-done.1
  53.6 1.9 %collective-permute-start.2 = (bf16[3072,128]{1,0:T(8,128)(2,1)}, bf16[3072,128]{1,0:T(8,128)(2,1)}, u32[]{:S(2)}, u32[]{:S(2)}) collective-permute-start(bf16[3072,128]{1,0:T(8,128)(2,1)} %collective-permute-done.1), channel_id=1, source_target_pairs={{0,0},{4,8},{8,4},{12,12},{1,1},{5,9},{9,5},{13,13},{2,2},{6,10},{... | collective-permute-start | bytes 2359304 | tf_op jit(solution)/shard_map/ppermute | solution.py:423
  55.6 0.0 collective-permute-done.6
  55.6 3.8 %collective-permute-start.7 = (bf16[3072,128]{1,0:T(8,128)(2,1)}, bf16[3072,128]{1,0:T(8,128)(2,1)S(1)}, u32[]{:S(2)}, u32[]{:S(2)}) collective-permute-start(bf16[3072,128]{1,0:T(8,128)(2,1)} %collective-permute-done.6), channel_id=1, source_target_pairs={{0,1},{1,0},{2,3},{3,2},{4,9},{5,8},{6,11},{7,10},{8,5},{9,4},{10,... | collective-permute-start | bytes 2359304 | tf_op jit(solution)/shard_map/ppermute | solution.py:37
  59.4 2.0 %multiply_convert_fusion.1 = (bf16[512,1024]{1,0:T(8,128)(2,1)S(1)}, bf16[512,1024]{1,0:T(8,128)(2,1)S(1)}) fusion(f32[512,1024]{1,0:T(8,128)S(1)} %get-tuple-element.26, f32[1024]{0:T(1024)S(1)} %get-tuple-element.48, f32[512]{0:T(512)S(1)} %add_rsqrt_fusion, f32[1024]{0:T(1024)S(1)} %get-tuple-element.49, f32[512,1024]{1,0:T(8,128)} %copy-done), kind=kLoop, calls=%fused_computation.3 | loop fusion | flops 3145728 | bytes 6301696 | tf_op jit(solution)/shard_map/convert_element_type | solution.py:377
  61.5 0.0 copy-start.12
  61.5 1.5 %pad_maximum_fusion = bf16[512,2048]{1,0:T(8,128)(2,1)} fusion(bf16[512,1024]{1,0:T(8,128)(2,1)S(1)} %get-tuple-element.51, bf16[512,1024]{1,0:T(8,128)(2,1)S(1)} %get-tuple-element.50), kind=kLoop, calls=%fused_computation | loop fusion | flops 4194304 | bytes 4194304 | tf_op jit(solution)/shard_map/concatenate | solution.py:379
  63.0 0.1 copy.25.cur_ref
  63.1 0.0 copy-start.1
  63.1 0.1 collective-permute-start.5
  63.2 0.0 collective-permute-done.4.sk_ref
  63.2 9.6 %collective-permute-done.2.pk_ref = bf16[3072,128]{1,0:T(8,128)(2,1)} collective-permute-done((bf16[3072,128]{1,0:T(8,128)(2,1)}, bf16[3072,128]{1,0:T(8,128)(2,1)}, u32[]{:S(2)}, u32[]{:S(2)}) %collective-permute-start.2) | collective-permute-done | bytes 786464 | tf_op jit(solution)/shard_map/ppermute | solution.py:423
  72.8 12.8 %weigh.1 = (bf16[2,512,3072]{2,1,0:T(8,128)(2,1)S(1)}, bf16[2,512,1024]{2,1,0:T(8,128)(2,1)S(1)}, f32[2,512,128]{2,1,0:T(8,128)S(1)}, f32[2,512,128]{2,1,0:T(8,128)S(1)}, bf16[4096,128]{1,0:T(8,128)(2,1)}) custom-call(bf16[2,512,128]{2,1,0:T(8,128)(2,1)S(1)} %bitcast.48, bf16[3072,128]{1,0:T(8,128)(2,1)} %collective-permute-done.2.pk_ref, ...), custom_call_target="tpu_custom_call" | custom-call | flops 2147483648 | bytes 16777216 | tf_op jit(solution)/shard_map/weigh/pallas_call | solution.py:157
  85.6 9.2 %collective-permute-done.7.v_ref = bf16[3072,128]{1,0:T(8,128)(2,1)S(1)} collective-permute-done((bf16[3072,128]{1,0:T(8,128)(2,1)}, bf16[3072,128]{1,0:T(8,128)(2,1)S(1)}, u32[]{:S(2)}, u32[]{:S(2)}) %collective-permute-start.7) | collective-permute-done | bytes 786464 | tf_op jit(solution)/shard_map/ppermute | solution.py:37
  94.8 3.0 %mix.1 = (f32[64,2048]{1,0:T(8,128)S(1)}, bf16[4096,128]{1,0:T(8,128)(2,1)}) custom-call(bf16[2,512,3072]{2,1,0:T(8,128)(2,1)S(1)} %get-tuple-element.39.w_ref, bf16[3072,128]{1,0:T(8,128)(2,1)S(1)} %collective-permute-done.7.v_ref, f32[2,512,128]{2,1,0:T(8,128)S(1)} %get-tuple-element.40.own_ref, f32[2,512,128]{2,1,0:T(8,128)S(1)} %get-tuple-element.41.inv_ref, ...), custom_call_target="tpu_custom_call" | custom-call | flops 1610612736 | bytes 8388608 | tf_op jit(solution)/shard_map/mix/pallas_call | solution.py:210
  97.7 0.0 collective-permute-done.5.v_ref.s_ref
  97.7 3.4 %close.1 = (f32[64,2048]{1,0:T(8,128)S(1)}, f32[8,128]{1,0:T(8,128)S(1)}) custom-call(bf16[2,512,1024]{2,1,0:T(8,128)(2,1)S(1)} %get-tuple-element.37.w_ref, bf16[1024,128]{1,0:T(8,128)(2,1)S(1)} %collective-permute-done.5.v_ref.s_ref, f32[64,2048]{1,0:T(8,128)S(1)} %get-tuple-element.42.part_ref, f32[2,512,128]{2,1,0:T(8,128)S(1)} %get-tuple-element.41.inv_ref), custom_call_target="tpu_custom_call" | custom-call | flops 536870912 | bytes 4194304 | tf_op jit(solution)/shard_map/close/pallas_call | solution.py:290
  101.1 0.9 write.1
  (19 shorter events, 0.1 us)
Async XLA Ops:
  0.6 7.0 %copy-start.6 = (bf16[1,512,2,128]{3,2,1,0:T(2,128)(2,1)S(1)}, bf16[1,512,2,128]{3,2,1,0:T(2,128)(2,1)}, u32[]{:S(2)}) copy-start(bf16[1,512,2,128]{3,2,1,0:T(2,128)(2,1)} %param.16) | copy-start | bytes 786436
  0.6 7.0 %copy-start.4 = (bf16[1,1536,2,128]{3,2,1,0:T(2,128)(2,1)S(1)}, bf16[1,1536,2,128]{3,2,1,0:T(2,128)(2,1)}, u32[]{:S(2)}) copy-start(bf16[1,1536,2,128]{3,2,1,0:T(2,128)(2,1)} %param.13) | copy-start | bytes 2359300
  0.7 43.3 %collective-permute-start = (bf16[1024,128]{1,0:T(8,128)(2,1)}, bf16[1024,128]{1,0:T(8,128)(2,1)S(1)}, u32[]{:S(2)}, u32[]{:S(2)}) collective-permute-start(bf16[1024,128]{1,0:T(8,128)(2,1)} %bitcast.61), channel_id=1, source_target_pairs={{0,5},{1,4},{2,7},{3,6},{4,13},{5,12},{6,15},{7,14},{8,1},{9,0},{1... | collective-permute-start | bytes 786440 | tf_op jit(solution)/shard_map/ppermute | solution.py:37
  3.6 50.1 %collective-permute-start.1 = (bf16[3072,128]{1,0:T(8,128)(2,1)}, bf16[3072,128]{1,0:T(8,128)(2,1)}, u32[]{:S(2)}, u32[]{:S(2)}) collective-permute-start(bf16[3072,128]{1,0:T(8,128)(2,1)} %bitcast.58), channel_id=1, source_target_pairs={{0,4},{4,12},{8,0},{12,8},{1,5},{5,13},{9,1},{13,9},{2,6},{6,14},{... | collective-permute-start | bytes 2359304 | tf_op jit(solution)/shard_map/ppermute | solution.py:407
  3.7 40.9 %collective-permute-start.3 = (bf16[1024,128]{1,0:T(8,128)(2,1)}, bf16[1024,128]{1,0:T(8,128)(2,1)}, u32[]{:S(2)}, u32[]{:S(2)}) collective-permute-start(bf16[1024,128]{1,0:T(8,128)(2,1)} %bitcast.62), channel_id=1, source_target_pairs={{0,4},{4,12},{8,0},{12,8},{1,5},{5,13},{9,1},{13,9},{2,6},{6,14},{... | collective-permute-start | bytes 786440 | tf_op jit(solution)/shard_map/ppermute | solution.py:407
  3.8 4.0 %copy-start.3 = (bf16[1,512,16,128]{3,2,1,0:T(8,128)(2,1)S(1)}, bf16[1,512,16,128]{3,2,1,0:T(8,128)(2,1)}, u32[]{:S(2)}) copy-start(bf16[1,512,16,128]{3,2,1,0:T(8,128)(2,1)} %param.14) | copy-start | bytes 6291460
  3.8 51.8 %collective-permute-start.6 = (bf16[3072,128]{1,0:T(8,128)(2,1)}, bf16[3072,128]{1,0:T(8,128)(2,1)}, u32[]{:S(2)}, u32[]{:S(2)}) collective-permute-start(bf16[3072,128]{1,0:T(8,128)(2,1)} %bitcast.59), channel_id=1, source_target_pairs={{0,5},{1,4},{2,7},{3,6},{4,13},{5,12},{6,15},{7,14},{8,1},{9,0},{1... | collective-permute-start | bytes 2359304 | tf_op jit(solution)/shard_map/ppermute | solution.py:37
  8.3 1.6 %copy-start.2 = (bf16[1,512,2048]{2,1,0:T(8,128)(2,1)S(1)}, bf16[1,512,2048]{2,1,0:T(8,128)(2,1)}, u32[]{:S(2)}) copy-start(bf16[1,512,2048]{2,1,0:T(8,128)(2,1)} %param.17) | copy-start | bytes 6291460
  26.1 17.6 %copy-start.9 = (bf16[2048]{0:T(1024)(128)(2,1)S(1)}, bf16[2048]{0:T(1024)(128)(2,1)}, u32[]{:S(2)}) copy-start(bf16[2048]{0:T(1024)(128)(2,1)} %param.23) | copy-start | bytes 12292
  26.1 17.6 %copy-start.5 = (bf16[1,2,32,16,128]{4,3,2,1,0:T(8,128)(2,1)S(1)}, bf16[1,2,32,16,128]{4,3,2,1,0:T(8,128)(2,1)}, u32[]{:S(2)}) copy-start(bf16[1,2,32,16,128]{4,3,2,1,0:T(8,128)(2,1)} %param.18) | copy-start | bytes 786436
  26.1 17.7 %copy-start.10 = (s32[1,32]{1,0:T(1,128)S(1)}, s32[1,32]{1,0:T(1,128)}, u32[]{:S(2)}) copy-start(s32[1,32]{1,0:T(1,128)} %param.22) | copy-start | bytes 388
  26.2 17.8 %copy-start.7 = (bf16[1,2,32,2,128]{4,3,2,1,0:T(2,128)(2,1)S(1)}, bf16[1,2,32,2,128]{4,3,2,1,0:T(2,128)(2,1)}, u32[]{:S(2)}) copy-start(bf16[1,2,32,2,128]{4,3,2,1,0:T(2,128)(2,1)} %param.20) | copy-start | bytes 98308
  26.2 17.8 %copy-start.8 = (bf16[1,2,32,2,128]{4,3,2,1,0:T(2,128)(2,1)S(1)}, bf16[1,2,32,2,128]{4,3,2,1,0:T(2,128)(2,1)}, u32[]{:S(2)}) copy-start(bf16[1,2,32,2,128]{4,3,2,1,0:T(2,128)(2,1)} %param.19) | copy-start | bytes 98308
  42.4 1.3 %copy-start = (f32[512,1024]{1,0:T(8,128)}, f32[512,1024]{1,0:T(8,128)S(1)}, u32[]{:S(2)}) copy-start(f32[512,1024]{1,0:T(8,128)S(1)} %get-tuple-element.30) | copy-start | bytes 6291460
  44.0 0.7 copy-start.11
  44.7 18.5 %collective-permute-start.4 = (bf16[1024,128]{1,0:T(8,128)(2,1)}, bf16[1024,128]{1,0:T(8,128)(2,1)S(1)}, u32[]{:S(2)}, u32[]{:S(2)}) collective-permute-start(bf16[1024,128]{1,0:T(8,128)(2,1)} %collective-permute-done.3), channel_id=1, source_target_pairs={{0,0},{4,8},{8,4},{12,12},{1,1},{5,9},{9,5},{13,13},{2,2},{6,10},{... | collective-permute-start | bytes 786440 | tf_op jit(solution)/shard_map/ppermute | solution.py:423
  53.6 19.2 %collective-permute-start.2 = (bf16[3072,128]{1,0:T(8,128)(2,1)}, bf16[3072,128]{1,0:T(8,128)(2,1)}, u32[]{:S(2)}, u32[]{:S(2)}) collective-permute-start(bf16[3072,128]{1,0:T(8,128)(2,1)} %collective-permute-done.1), channel_id=1, source_target_pairs={{0,0},{4,8},{8,4},{12,12},{1,1},{5,9},{9,5},{13,13},{2,2},{6,10},{... | collective-permute-start | bytes 2359304 | tf_op jit(solution)/shard_map/ppermute | solution.py:423
  55.6 39.2 %collective-permute-start.7 = (bf16[3072,128]{1,0:T(8,128)(2,1)}, bf16[3072,128]{1,0:T(8,128)(2,1)S(1)}, u32[]{:S(2)}, u32[]{:S(2)}) collective-permute-start(bf16[3072,128]{1,0:T(8,128)(2,1)} %collective-permute-done.6), channel_id=1, source_target_pairs={{0,1},{1,0},{2,3},{3,2},{4,9},{5,8},{6,11},{7,10},{8,5},{9,4},{10,... | collective-permute-start | bytes 2359304 | tf_op jit(solution)/shard_map/ppermute | solution.py:37
  61.5 1.6 %copy-start.12 = (bf16[1024,128]{1,0:T(8,128)(2,1)S(1)}, bf16[1024,128]{1,0:T(8,128)(2,1)}, u32[]{:S(2)}) copy-start(bf16[1024,128]{1,0:T(8,128)(2,1)} %copy-done.11) | copy-start | bytes 786436
  63.1 31.7 %copy-start.1 = (bf16[1,2,32,2048]{3,2,1,0:T(8,128)(2,1)S(1)}, bf16[1,2,32,2048]{3,2,1,0:T(8,128)(2,1)}, u32[]{:S(2)}) copy-start(bf16[1,2,32,2048]{3,2,1,0:T(8,128)(2,1)} %param.21) | copy-start | bytes 786436
  63.1 34.6 %collective-permute-start.5 = (bf16[1024,128]{1,0:T(8,128)(2,1)S(1)}, bf16[1024,128]{1,0:T(8,128)(2,1)S(1)}, u32[]{:S(2)}, u32[]{:S(2)}) collective-permute-start(bf16[1024,128]{1,0:T(8,128)(2,1)S(1)} %copy-done.12), channel_id=1, source_target_pairs={{0,1},{1,0},{2,3},{3,2},{4,9},{5,8},{6,11},{7,10},{8,5},{9,4},{10,... | collective-permute-start | bytes 786440 | tf_op jit(solution)/shard_map/ppermute | solution.py:37
